TPU v7x, 32 devices: a whole 2x2x4 slice. The times are simulated.
32 devices in a mesh: dp: 8 (over z, x), tensor: 4 (over y, core).
Axes of the slice: x: 2, y: 2, z: 4, core: 2. Of those that a mesh axis runs over, the one named last changes fastest.
Arguments:
- tokens: bfloat16 [8, 256, 4096], P('dp', 'tensor'), may hold values from -6 to 6
- gain: bfloat16 [4096], replicated, may hold values from 0.5 to 1.5
- wq: bfloat16 [4096, 4096], P(None, 'tensor'), may hold values from -0.09375 to 0.09375
- bq: bfloat16 [4096], P('tensor'), may hold values from -5 to 5
- wkv: bfloat16 [4096, 1024], P(None, 'tensor'), may hold values from -0.09375 to 0.09375
- bkv: bfloat16 [1024], P('tensor'), may hold values from -5 to 5
- wo: bfloat16 [4096, 4096], P('tensor'), may hold values from -0.375 to 0.375
- check_weights: float32 [8, 256], P('dp'), may hold values from -12 to 12
Outputs:
- attended: bfloat16 [8, 256, 4096], P('dp', 'tensor')
- checksum: float32 [4096], replicated
All inputs are finite; a program needn't handle non-finite values.
Results may differ from a plain program's by a relative error of at most 0.018.
Values may be sent and summed in bfloat16 or wider, within the bound.
A program may use at most 64 MiB of HBM per device.

v0:
```python
import jax
import jax.numpy as jnp
from jax import lax
from jax.sharding import PartitionSpec as P

HEADS = 32
KV = 4
HD = 128
EPS = 1e-06
THETA = 1000000.0


def rope(values, head_size):
    rows = values.shape[0]
    half = head_size // 2
    inverse = THETA ** (-(jnp.arange(half, dtype=jnp.float32) * 2.0 / head_size))
    angles = jnp.arange(rows, dtype=jnp.float32)[:, None] * inverse[None, :]
    cosine = jnp.cos(angles)[:, None, :]
    sine = jnp.sin(angles)[:, None, :]
    shaped = values.reshape(rows, -1, head_size)
    first = shaped[..., :half]
    second = shaped[..., half:]
    turned = jnp.concatenate(
        [first * cosine - second * sine, second * cosine + first * sine], axis=-1
    )
    return turned.reshape(rows, -1)


def local(tokens, gain, wq, bq, wkv, bkv, wo, check_weights):
    states = tokens[0].astype(jnp.float32)
    normed = (
        states
        * lax.rsqrt(jnp.mean(states * states, axis=-1, keepdims=True) + EPS)
        * gain.astype(jnp.float32)
    ).astype(jnp.bfloat16)
    position = lax.axis_index("tensor")
    head_dev = wq.shape[1] // HD
    query_cols = head_dev * HD
    shared = position * head_dev // (HEADS // KV)
    joined_w = jnp.concatenate([wq, wkv], axis=1)
    joined_b = jnp.concatenate([bq, bkv], axis=0).astype(jnp.float32)
    projected = (
        jnp.dot(
            lax.all_gather(normed, "tensor", axis=0, tiled=True),
            joined_w,
            preferred_element_type=jnp.float32,
        )
        + joined_b[None, :]
    )
    seq_rows = projected.shape[0]
    query = rope(projected[:, :query_cols], HD).astype(jnp.bfloat16)
    kv_local = projected[:, query_cols:].astype(jnp.bfloat16)
    kv_whole = lax.all_gather(kv_local, "tensor", axis=1, tiled=True)
    key_part = lax.dynamic_slice_in_dim(kv_whole, shared * HD, HD, 1)
    values = lax.dynamic_slice_in_dim(kv_whole, KV * HD + shared * HD, HD, 1)
    keys = rope(key_part.astype(jnp.float32), HD).astype(jnp.bfloat16)
    scale = HD ** (-0.5)
    block = min(512, seq_rows)
    query_heads = query.reshape(seq_rows, head_dev, HD)
    pieces = []
    for number in range(seq_rows // block):
        stop = (number + 1) * block
        query_block = query_heads[number * block : stop]
        scores = (
            jnp.einsum("qhd,kd->hqk", query_block, keys[:stop], preferred_element_type=jnp.float32)
            * scale
        )
        allowed = jnp.arange(block)[:, None] + number * block >= jnp.arange(stop)[None, :]
        scores = jnp.where(allowed[None, :, :], scores, -1e30)
        probs = jax.nn.softmax(scores, axis=-1).astype(jnp.bfloat16)
        mixed = jnp.einsum(
            "hqk,kd->qhd", probs, values[:stop], preferred_element_type=jnp.float32
        ).astype(jnp.bfloat16)
        pieces.append(mixed.reshape(block, query_cols))
    context = jnp.concatenate(pieces, axis=0)
    summed = lax.psum_scatter(
        jnp.dot(context, wo, preferred_element_type=jnp.float32).astype(jnp.bfloat16),
        "tensor",
        scatter_dimension=0,
        tiled=True,
    )
    attended = summed[None, :, :]
    summary = jnp.dot(
        check_weights[0], context.astype(jnp.float32), precision=lax.Precision.HIGHEST
    )
    term = jnp.dot(summary, wo.astype(jnp.float32), precision=lax.Precision.HIGHEST)
    total = lax.psum(term, ("dp", "tensor"))
    checksum = total / jnp.sqrt(jnp.float32(seq_rows * lax.axis_size("dp")))
    return (attended, checksum)


def solution(mesh):
    placed = (
        P("dp", "tensor", None),
        P(),
        P(None, "tensor"),
        P("tensor"),
        P(None, "tensor"),
        P("tensor"),
        P("tensor", None),
        P("dp", None),
    )
    return jax.shard_map(
        local, mesh=mesh, in_specs=placed, out_specs=(P("dp", "tensor", None), P()), check_vma=False
    )
```

profile of v0, /device:TPU:0, one launch (start us, length us, event | category | flops | bytes accessed | tf_op | source)
XLA Modules:
  0.0 118.1 jit_solution(9520385289400516932)
XLA Ops:
  7.2 0.0 copy-start
  7.2 0.0 all-gather.2.cloned.1.call-start
  7.3 0.8 convert_element_type.43
  8.1 1.2 %fusion.9 = f32[64]{0:T(128)S(1)} fusion(bf16[1,64,4096]{2,1,0:T(8,128)(2,1)} %param.8), kind=kLoop, calls=%fused_computation.15 | loop fusion | flops 786368 | bytes 524544 | tf_op jit(solution)/shard_map/reduce_sum | solution.py:33
  9.4 2.0 %fusion.11 = bf16[64,4096]{1,0:T(8,128)(2,1)} fusion(bf16[1,64,4096]{2,1,0:T(8,128)(2,1)} %param.8, f32[4096]{0:T(1024)S(1)} %convert_element_type.43, f32[64]{0:T(128)S(1)} %add_rsqrt_fusion), kind=kLoop, calls=%fused_computation.17 | loop fusion | flops 1048576 | bytes 1065216 | tf_op jit(solution)/shard_map/convert_element_type | solution.py:35
  11.4 0.0 all-gather.2.cloned.1.call-update
  11.4 0.0 reduce-scatter.2.cloned.1.call-start
  11.6 0.5 fusion.24
  12.1 24.8 %all-gather.2.cloned.1.call-done = bf16[256,4096]{1,0:T(8,128)(2,1)} async-done(((bf16[64,4096]{1,0:T(8,128)(2,1)}), bf16[256,4096]{1,0:T(8,128)(2,1)}) %all-gather.2.cloned.1.call-update) | async-done | bytes 2097168 | tf_op jit(solution)/shard_map/all_gather | solution.py:44
  36.9 7.5 %fusion.5 = f32[256,1280]{1,0:T(8,128)S(1)} fusion(bf16[256,4096]{1,0:T(8,128)(2,1)} %all-gather.2.cloned.1.call-done, bf16[4096,256]{1,0:T(8,128)(2,1)S(1)} %copy-done.3, bf16[4096,1024]{1,0:T(8,128)(2,1)} %param.10, f32[1280]{0:T(1024)S(1)} %maximum_convert_fusion), kind=kOutput, calls=%fused_computation.6 | convolution fusion | flops 2705653760 | bytes 13898752 | tf_op jit(solution)/shard_map/dot_general | solution.py:43
  44.4 0.1 slice_bitcast_fusion
  44.5 7.2 %all_gather.7 = bf16[256,1024]{1,0:T(8,128)(2,1)S(1)} all-gather(bf16[256,256]{1,0:T(8,128)(2,1)S(1)} %slice.37), channel_id=1, replica_groups=mesh['dp'=8,'tensor'=4] {'tensor'}, dimensions={1}, use_global_device_ids=true | all-gather | bytes 655360 | tf_op jit(solution)/shard_map/all_gather | solution.py:53
  51.7 0.5 subtract_convert_fusion.1
  52.3 0.2 copy.19
  52.5 0.3 fusion.39
  52.8 0.4 subtract_convert_fusion
  53.2 2.4 %fusion.40 = (f32[8,256]{1,0:T(8,128)S(1)}, f32[8,256,256]{1,2,0:T(8,128)}) fusion(pred[256,256]{0,1:T(8,128)(4,1)S(1)} %iota_compare_fusion, bf16[256,8,64]{2,0,1:T(8,128)(2,1)S(1)} %get-tuple-element.3, bf16[256,8,64]{2,0,1:T(8,128)(2,1)S(1)} %get-tuple-element.2, bf16[256,1,64]{2,0,1:T(8,128)(2,1)S(1)} %get-tuple-element.7, ...), kind=kOutput, calls=%fused_computation.54 | convolution fusion | flops 137494784 | bytes 2760704 | tf_op jit(solution)/shard_map/sub | solution.py:70
  55.6 1.9 %convolution_convert_fusion.1 = bf16[128,8,256]{2,0,1:T(8,128)(2,1)S(1)} fusion(f32[8,256,256]{1,2,0:T(8,128)} %get-tuple-element.11, f32[8,256]{1,0:T(8,128)S(1)} %get-tuple-element.10, bf16[256,1024]{1,0:T(8,128)(2,1)S(1)} %all_gather.7, s32[]{:T(128)S(6)} %select_n.16), kind=kOutput, calls=%fused_computation.13 | convolution fusion | flops 135528448 | bytes 2695172 | tf_op jit(solution)/shard_map/hqk,kd->qhd/dot_general | solution.py:71
  57.5 7.1 %convolution_convert_fusion = bf16[256,4096]{1,0:T(8,128)(2,1)} fusion(bf16[256,1024]{0,1:T(8,128)(2,1)S(1)} %bitcast.49, bf16[1024,4096]{1,0:T(8,128)(2,1)} %param.14), kind=kOutput, calls=%fused_computation.5 | convolution fusion | flops 2148532224 | bytes 11010048 | tf_op jit(solution)/shard_map/dot_general | solution.py:77
  64.6 0.0 reduce-scatter.2.cloned.1.call-update
  64.7 0.5 convolution_bitcast_fusion
  65.2 5.7 %fusion.43 = f32[1,4096]{1,0:T(1,128)S(1)} fusion(f32[1024,1]{0,1:T(1,128)S(1)} %convolution_bitcast_fusion, bf16[1024,4096]{1,0:T(8,128)(2,1)} %param.14), kind=kOutput, calls=%fused_computation.55 | convolution fusion | flops 50331648 | bytes 8409088 | tf_op jit(solution)/shard_map/dot_general | solution.py:86
  70.9 39.7 %psum.7 = f32[4096]{0:T(1024)S(1)} all-reduce(f32[4096]{0:T(1024)S(1)} %bitcast.51), channel_id=1, replica_groups=mesh['dp'=8,'tensor'=4] {'dp','tensor'}, use_global_device_ids=true, to_apply=%region_4.5 | all-reduce | flops 4096 | bytes 32768 | tf_op jit(solution)/shard_map/psum | solution.py:87
  110.6 0.6 broadcast_multiply_fusion
  (14 shorter events, 0.1 us)
Async XLA Ops:
  7.2 57.5 %copy-start = (f32[1,256]{1,0:T(1,128)S(1)}, f32[1,256]{1,0:T(1,128)}, u32[]{:S(2)}) copy-start(f32[1,256]{1,0:T(1,128)} %param.15) | copy-start | bytes 3076
  7.2 4.3 %copy-start.1 = (bf16[1024]{0:T(1024)(128)(2,1)S(1)}, bf16[1024]{0:T(1024)(128)(2,1)}, u32[]{:S(2)}) copy-start(bf16[1024]{0:T(1024)(128)(2,1)} %param.11) | copy-start | bytes 6148
  7.2 4.3 %copy-start.2 = (bf16[256]{0:T(256)(128)(2,1)S(1)}, bf16[256]{0:T(256)(128)(2,1)}, u32[]{:S(2)}) copy-start(bf16[256]{0:T(256)(128)(2,1)} %param.13) | copy-start | bytes 1540
  7.2 29.7 %copy-start.3 = (bf16[4096,256]{1,0:T(8,128)(2,1)S(1)}, bf16[4096,256]{1,0:T(8,128)(2,1)}, u32[]{:S(2)}) copy-start(bf16[4096,256]{1,0:T(8,128)(2,1)} %param.12) | copy-start | bytes 6291460
  7.2 29.7 %all-gather.2.cloned.1.call-start = ((), (), s32[]{:S(2)}) async-start(), calls=%async_computation.1 | async-start | bytes 2621440 | tf_op jit(solution)/shard_map/all_gather | solution.py:44
  11.4 99.8 %reduce-scatter.2.cloned.1.call-start = ((), (), s32[]{:S(2)}) async-start(), calls=%async_computation.2 | async-start | bytes 2621440 | tf_op jit(solution)/shard_map/reduce_scatter | solution.py:76
Sparse Core Ops, SparseCore 0:
  11.5 25.2 all-gather.1
  64.8 31.3 reduce-scatter.1
where the time goes:
time: 118 us
  blocking collectives  46.9 us (40%)
  matrix products  25.1 us (21%)
  waiting for transfers between devices  24.8 us (21%)
  between operations  14.2 us (12%)
  other arithmetic  6.25 us (5%)
    psum x1, blocking collectives, local(): total = lax.psum(term, ('dp', 'tensor'))  39.7 us
    all_gather x1, waiting for transfers between devices, local(): lax.all_gather(normed, 'tensor', axis=0, tiled=True)  24.8 us
    dot_general x1, matrix products, local(): jnp.dot(lax.all_gather(normed, 'tensor', axis=0, tiled=True), joined_w, p...  7.53 us
    all_gather x1, blocking collectives, local(): kv_whole = lax.all_gather(kv_local, 'tensor', axis=1, tiled=True)  7.16 us
    dot_general x1, matrix products, local(): jnp.dot(context, wo, preferred_element_type=jnp.float32)  7.11 us
    dot_general x1, matrix products, local(): jnp.dot(summary, wo.astype(jnp.float32), precision=lax.Precision.HIGHEST)  5.68 us
  transfers between devices with their start and end apart: 2, of which 1 were waited for; matrix products, arithmetic and copies ran while one was open for 6% of the time, Pallas kernels for 0%

commit v1 on v0

--- a/solution.py
+++ b/solution.py
@@ -2,6 +2,7 @@
 import jax.numpy as jnp
 from jax import lax
 from jax.sharding import PartitionSpec as P
+from jax.lax import axis_index, axis_size, ppermute
 
 HEADS = 32
 KV = 4
@@ -27,6 +28,20 @@
 
 
 def local(tokens, gain, wq, bq, wkv, bkv, wo, check_weights):
+
+    def supply_all_indices(mine_x, bus_axis):
+        n_dev_all = axis_size(bus_axis)
+        h_now = [(k - 1, k) for k in range(1, n_dev_all)] + [(n_dev_all - 1, 0)]
+        back = mine_x
+        j = 0
+        frames = [back]
+        while j < n_dev_all - 1:
+            back = ppermute(back, bus_axis, h_now)
+            frames += [back]
+            j += 1
+        spare = jnp.concatenate([*reversed(frames)], 1)
+        return jnp.roll(spare, shift=(axis_index(bus_axis) + 1) * back.shape[1], axis=1)
+
     states = tokens[0].astype(jnp.float32)
     normed = (
         states
@@ -50,7 +65,7 @@
     seq_rows = projected.shape[0]
     query = rope(projected[:, :query_cols], HD).astype(jnp.bfloat16)
     kv_local = projected[:, query_cols:].astype(jnp.bfloat16)
-    kv_whole = lax.all_gather(kv_local, "tensor", axis=1, tiled=True)
+    kv_whole = supply_all_indices(kv_local, "tensor")
     key_part = lax.dynamic_slice_in_dim(kv_whole, shared * HD, HD, 1)
     values = lax.dynamic_slice_in_dim(kv_whole, KV * HD + shared * HD, HD, 1)
     keys = rope(key_part.astype(jnp.float32), HD).astype(jnp.bfloat16)

time: 118 us -> 124 us (1.051)
  waiting for transfers between devices: 24.8 us -> 36.7 us
  blocking collectives: 46.9 us -> 39.8 us
    ppermute x0 -> x3, waiting for transfers between devices: none -> 11.9 us  [supply_all_indices(): back = ppermute(back, bus_axis, h_now)]
    all_gather x1 -> x0, blocking collectives: 7.16 us -> none  [local(): kv_whole = lax.all_gather(kv_local, 'tensor', axis=1, tiled=True)]
  transfers between devices with their start and end apart: 2 -> 5, of which waited for: 1 -> 4; matrix products, arithmetic and copies ran while one was open for 6% -> 7% of each run, Pallas kernels for 0% -> 0%
where the time goes in v1:
time: 124 us; the launch traced here: 123 us
  blocking collectives  39.8 us (32%)
  waiting for transfers between devices  36.7 us (30%)
  matrix products  25.2 us (20%)
  between operations  14.3 us (12%)
  other arithmetic  6.33 us (5%)
    psum x1, blocking collectives, local(): total = lax.psum(term, ('dp', 'tensor'))  39.8 us
    all_gather x1, waiting for transfers between devices, local(): lax.all_gather(normed, 'tensor', axis=0, tiled=True)  24.8 us
    ppermute x3, waiting for transfers between devices, supply_all_indices(): back = ppermute(back, bus_axis, h_now)  11.9 us
    dot_general x1, matrix products, local(): jnp.dot(lax.all_gather(normed, 'tensor', axis=0, tiled=True), joined_w, p...  7.53 us
    dot_general x1, matrix products, local(): jnp.dot(context, wo, preferred_element_type=jnp.float32)  7.1 us
    dot_general x1, matrix products, local(): jnp.dot(summary, wo.astype(jnp.float32), precision=lax.Precision.HIGHEST)  5.68 us
  transfers between devices with their start and end apart: 5, of which 4 were waited for; matrix products, arithmetic and copies ran while one was open for 7% of the time, Pallas kernels for 0%

profile of v1, /device:TPU:0, one launch (start us, length us, event | category | flops | bytes accessed | tf_op | source)
XLA Modules:
  0.0 123.4 jit_solution(10739767924785312487)
XLA Ops:
  7.3 0.8 convert_element_type.43
  8.1 1.2 %fusion.9 = f32[64]{0:T(128)S(1)} fusion(bf16[1,64,4096]{2,1,0:T(8,128)(2,1)} %param.8), kind=kLoop, calls=%fused_computation.15 | loop fusion | flops 786368 | bytes 524544 | tf_op jit(solution)/shard_map/reduce_sum | solution.py:48
  9.4 2.0 %fusion.11 = bf16[64,4096]{1,0:T(8,128)(2,1)} fusion(bf16[1,64,4096]{2,1,0:T(8,128)(2,1)} %param.8, f32[4096]{0:T(1024)S(1)} %convert_element_type.43, f32[64]{0:T(128)S(1)} %add_rsqrt_fusion), kind=kLoop, calls=%fused_computation.17 | loop fusion | flops 1048576 | bytes 1065216 | tf_op jit(solution)/shard_map/convert_element_type | solution.py:50
  11.4 0.0 reduce-scatter.2.cloned.1.call-start
  11.6 0.5 fusion.24
  12.1 24.8 %all-gather.2.cloned.1.call-done = bf16[256,4096]{1,0:T(8,128)(2,1)} async-done(((bf16[64,4096]{1,0:T(8,128)(2,1)}), bf16[256,4096]{1,0:T(8,128)(2,1)}) %all-gather.2.cloned.1.call-update) | async-done | bytes 2097168 | tf_op jit(solution)/shard_map/all_gather | solution.py:59
  36.9 7.5 %fusion.5 = f32[256,1280]{1,0:T(8,128)S(1)} fusion(bf16[256,4096]{1,0:T(8,128)(2,1)} %all-gather.2.cloned.1.call-done, bf16[4096,256]{1,0:T(8,128)(2,1)S(1)} %copy-done.3, bf16[4096,1024]{1,0:T(8,128)(2,1)} %param.10, f32[1280]{0:T(1024)S(1)} %maximum_convert_fusion), kind=kOutput, calls=%fused_computation.6 | convolution fusion | flops 2705653760 | bytes 13898752 | tf_op jit(solution)/shard_map/dot_general | solution.py:58
  44.4 0.3 collective-permute-start
  44.7 0.1 slice_bitcast_fusion
  44.8 0.2 copy.19
  45.0 3.8 %collective-permute-done = bf16[256,256]{1,0:T(8,128)(2,1)S(1)} collective-permute-done((bf16[256,256]{1,0:T(8,128)(2,1)S(1)}, bf16[256,256]{1,0:T(8,128)(2,1)S(1)}, u32[]{:S(2)}, u32[]{:S(2)}) %collective-permute-start) | collective-permute-done | bytes 131104 | tf_op jit(solution)/shard_map/ppermute | solution.py:39
  48.9 0.3 fusion.39
  49.2 4.1 %collective-permute-done.1 = bf16[256,256]{1,0:T(8,128)(2,1)S(1)} collective-permute-done((bf16[256,256]{1,0:T(8,128)(2,1)S(1)}, bf16[256,256]{1,0:T(8,128)(2,1)S(1)}, u32[]{:S(2)}, u32[]{:S(2)}) %collective-permute-start.1) | collective-permute-done | bytes 131104 | tf_op jit(solution)/shard_map/ppermute | solution.py:39
  53.3 0.4 subtract_convert_fusion
  53.7 4.0 %collective-permute-done.2 = bf16[256,256]{1,0:T(8,128)(2,1)S(1)} collective-permute-done((bf16[256,256]{1,0:T(8,128)(2,1)S(1)}, bf16[256,256]{1,0:T(8,128)(2,1)S(1)}, u32[]{:S(2)}, u32[]{:S(2)}) %collective-permute-start.2) | collective-permute-done | bytes 131104 | tf_op jit(solution)/shard_map/ppermute | solution.py:39
  57.8 0.1 bitcast_convert_fusion
  57.9 0.5 subtract_convert_fusion.1
  58.5 2.3 %fusion.40 = (f32[8,256]{1,0:T(8,128)S(1)}, f32[8,256,256]{1,2,0:T(8,128)}) fusion(pred[256,256]{0,1:T(8,128)(4,1)S(1)} %iota_compare_fusion, bf16[256,8,64]{2,0,1:T(8,128)(2,1)S(1)} %get-tuple-element.3, bf16[256,8,64]{2,0,1:T(8,128)(2,1)S(1)} %get-tuple-element.2, bf16[256,1,64]{2,0,1:T(8,128)(2,1)S(1)} %get-tuple-element.7, ...), kind=kOutput, calls=%fused_computation.62 | convolution fusion | flops 137494784 | bytes 2760704 | tf_op jit(solution)/shard_map/sub | solution.py:85
  60.8 2.0 %convolution_convert_fusion.1 = bf16[128,8,256]{2,0,1:T(8,128)(2,1)S(1)} fusion(f32[8,256,256]{1,2,0:T(8,128)} %get-tuple-element.11, f32[8,256]{1,0:T(8,128)S(1)} %get-tuple-element.10, bf16[256,2048]{1,0:T(8,128)(2,1)S(1)} %constant_dynamic-update-slice_fusion, s32[]{:T(128)S(6)} %dynamic_slice.14), kind=kOutput, calls=%fused_computation.13 | convolution fusion | flops 135528448 | bytes 2695172 | tf_op jit(solution)/shard_map/hqk,kd->qhd/dot_general | solution.py:86
  62.8 7.1 %convolution_convert_fusion = bf16[256,4096]{1,0:T(8,128)(2,1)} fusion(bf16[256,1024]{0,1:T(8,128)(2,1)S(1)} %bitcast.49, bf16[1024,4096]{1,0:T(8,128)(2,1)} %param.14), kind=kOutput, calls=%fused_computation.5 | convolution fusion | flops 2148532224 | bytes 11010048 | tf_op jit(solution)/shard_map/dot_general | solution.py:92
  69.9 0.5 convolution_bitcast_fusion
  70.5 5.7 %fusion.43 = f32[1,4096]{1,0:T(1,128)S(1)} fusion(f32[1024,1]{0,1:T(1,128)S(1)} %convolution_bitcast_fusion, bf16[1024,4096]{1,0:T(8,128)(2,1)} %param.14), kind=kOutput, calls=%fused_computation.63 | convolution fusion | flops 50331648 | bytes 8409088 | tf_op jit(solution)/shard_map/dot_general | solution.py:101
  76.1 39.8 %psum.7 = f32[4096]{0:T(1024)S(1)} all-reduce(f32[4096]{0:T(1024)S(1)} %bitcast.51), channel_id=1, replica_groups=mesh['dp'=8,'tensor'=4] {'dp','tensor'}, use_global_device_ids=true, to_apply=%region_4.5 | all-reduce | flops 4096 | bytes 32768 | tf_op jit(solution)/shard_map/psum | solution.py:102
  115.9 0.6 broadcast_multiply_fusion
  (27 shorter events, 0.3 us)
Async XLA Ops:
  7.2 62.8 %copy-start = (f32[1,256]{1,0:T(1,128)S(1)}, f32[1,256]{1,0:T(1,128)}, u32[]{:S(2)}) copy-start(f32[1,256]{1,0:T(1,128)} %param.15) | copy-start | bytes 3076
  7.2 4.3 %copy-start.1 = (bf16[1024]{0:T(1024)(128)(2,1)S(1)}, bf16[1024]{0:T(1024)(128)(2,1)}, u32[]{:S(2)}) copy-start(bf16[1024]{0:T(1024)(128)(2,1)} %param.11) | copy-start | bytes 6148
  7.2 4.3 %copy-start.2 = (bf16[256]{0:T(256)(128)(2,1)S(1)}, bf16[256]{0:T(256)(128)(2,1)}, u32[]{:S(2)}) copy-start(bf16[256]{0:T(256)(128)(2,1)} %param.13) | copy-start | bytes 1540
  7.2 29.7 %copy-start.3 = (bf16[4096,256]{1,0:T(8,128)(2,1)S(1)}, bf16[4096,256]{1,0:T(8,128)(2,1)}, u32[]{:S(2)}) copy-start(bf16[4096,256]{1,0:T(8,128)(2,1)} %param.12) | copy-start | bytes 6291460
  7.2 29.7 %all-gather.2.cloned.1.call-start = ((), (), s32[]{:S(2)}) async-start(), calls=%async_computation.1 | async-start | bytes 2621440 | tf_op jit(solution)/shard_map/all_gather | solution.py:59
  11.4 105.1 %reduce-scatter.2.cloned.1.call-start = ((), (), s32[]{:S(2)}) async-start(), calls=%async_computation.2 | async-start | bytes 2621440 | tf_op jit(solution)/shard_map/reduce_scatter | solution.py:91
  44.4 4.4 %collective-permute-start = (bf16[256,256]{1,0:T(8,128)(2,1)S(1)}, bf16[256,256]{1,0:T(8,128)(2,1)S(1)}, u32[]{:S(2)}, u32[]{:S(2)}) collective-permute-start(bf16[256,256]{1,0:T(8,128)(2,1)S(1)} %slice.37), channel_id=1, source_target_pairs={{0,1},{1,2},{2,3},{3,0},{4,5},{5,6},{6,7},{7,4},{8,9},{9,10},{10,1... | collective-permute-start | bytes 393224 | tf_op jit(solution)/shard_map/ppermute | solution.py:39
  48.9 4.4 %collective-permute-start.1 = (bf16[256,256]{1,0:T(8,128)(2,1)S(1)}, bf16[256,256]{1,0:T(8,128)(2,1)S(1)}, u32[]{:S(2)}, u32[]{:S(2)}) collective-permute-start(bf16[256,256]{1,0:T(8,128)(2,1)S(1)} %collective-permute-done), channel_id=1, source_target_pairs={{0,1},{1,2},{2,3},{3,0},{4,5},{5,6},{6,7},{7,4},{8,9},{9,10},{10,1... | collective-permute-start | bytes 393224 | tf_op jit(solution)/shard_map/ppermute | solution.py:39
  53.3 4.4 %collective-permute-start.2 = (bf16[256,256]{1,0:T(8,128)(2,1)S(1)}, bf16[256,256]{1,0:T(8,128)(2,1)S(1)}, u32[]{:S(2)}, u32[]{:S(2)}) collective-permute-start(bf16[256,256]{1,0:T(8,128)(2,1)S(1)} %collective-permute-done.1), channel_id=1, source_target_pairs={{0,1},{1,2},{2,3},{3,0},{4,5},{5,6},{6,7},{7,4},{8,9},{9,10},{10,1... | collective-permute-start | bytes 393224 | tf_op jit(solution)/shard_map/ppermute | solution.py:39
Sparse Core Ops, SparseCore 0:
  11.5 25.2 all-gather.1
  70.1 31.3 reduce-scatter.1
